TPU v7x, 32 devices: a whole 2x2x4 slice. The times are simulated.
32 devices in a mesh: groups: 2 (over x), kvseq: 8 (over z, y), tensor: 2 (over core).
Axes of the slice: x: 2, y: 2, z: 4, core: 2. Of those that a mesh axis runs over, the one named last changes fastest.
Arguments:
- hidden: bfloat16 [16, 8192], P('groups', 'kvseq'), parts along dimension 0, may hold values from -30 to 30
- lengths: int32 [16], P('groups'), parts along dimension 0, may hold values from 128 to 2048, as said below
- key_cache: bfloat16 [16, 2048, 1024], P('groups', 'kvseq', 'tensor'), parts along dimension 0, may hold values from -400 to 400
- value_cache: bfloat16 [16, 2048, 1024], P('groups', 'kvseq', 'tensor'), parts along dimension 0, may hold values from -60 to 60
- gain_in: float32 [8192], P('kvseq'), may hold values from 0.1 to 1.9
- w_query: bfloat16 [8192, 8192], P('kvseq', 'tensor'), may hold values from -0.0625 to 0.0625
- w_key: bfloat16 [8192, 1024], P('kvseq', 'tensor'), may hold values from -0.0625 to 0.0625
- w_value: bfloat16 [8192, 1024], P('kvseq', 'tensor'), may hold values from -0.0625 to 0.0625
- w_output: bfloat16 [8192, 8192], P('tensor', 'kvseq'), may hold values from -0.0625 to 0.0625
- gain_post: float32 [8192], P('kvseq'), may hold values from 0.1 to 1.9
- w_gate: bfloat16 [8192, 15360], P('kvseq', 'tensor'), may hold values from -0.0625 to 0.0625
- w_up: bfloat16 [8192, 15360], P('kvseq', 'tensor'), may hold values from -0.0625 to 0.0625
- w_down: bfloat16 [15360, 8192], P('tensor', 'kvseq'), may hold values from -0.046875 to 0.046875
Outputs:
- output: bfloat16 [16, 8192], P('groups', 'kvseq'), parts along dimension 0
- new_keys: bfloat16 [16, 1024], P('groups', 'tensor'), parts along dimension 0
- new_values: bfloat16 [16, 1024], P('groups', 'tensor'), parts along dimension 0
There are 2 independent parts, one for each index of `groups`. A program takes and returns all parts, laid end to end along the dimension named above; an argument that names none is the same for every part. Nothing has to cross between parts.
Inputs may be any that keep to these rules, and one draw needn't show every extreme that they name: `lengths`: multiples of 128; some sequence holds exactly 2048.
All inputs are finite; a program needn't handle non-finite values.
Results may differ from a plain program's by a relative error of at most 0.024.
Values may be sent and summed in bfloat16 or wider, within the bound.
A program may use at most 128 MiB of HBM per device.

v0:
```python
import jax
import jax.numpy as jnp
from jax import lax
from jax.sharding import PartitionSpec as P

D = 8192
HD = 128


epsilon = 1e-06
rope_base = 1000000.0


def combined_all(x, axis, join):
    gathered = jax.tree.map(
        lambda a, kind: lax.all_gather(a.astype(kind), axis),
        x,
        (jnp.bfloat16, jnp.bfloat16, jnp.bfloat16),
    )

    def take(source):
        return jax.tree.map(
            lambda a, own: lax.dynamic_index_in_dim(a, source, 0, False).astype(own.dtype),
            gathered,
            x,
        )

    return lax.fori_loop(
        1, lax.axis_size(axis), lambda source, state: join(state, take(source)), take(0)
    )


def rotate(values, position):
    half_dim = values.shape[-1] // 2
    frequency = rope_base ** (-jnp.arange(half_dim, dtype=jnp.float32) * 2.0 / values.shape[-1])
    angles = position[:, None, None] * frequency
    cosine = jnp.cos(angles)
    sine = jnp.sin(angles)
    lower = values[..., :half_dim]
    upper = values[..., half_dim:]
    return jnp.concatenate([lower * cosine - upper * sine, upper * cosine + lower * sine], axis=-1)


def combine_parts(earlier, later_part):
    top = jnp.maximum(earlier[0], later_part[0])
    scale_one = jnp.exp(earlier[0] - top)
    scale_two = jnp.exp(later_part[0] - top)
    total = earlier[1] * scale_one + later_part[1] * scale_two
    mixed = earlier[2] * scale_one[..., None] + later_part[2] * scale_two[..., None]
    return (top, total, mixed)


def per_device(
    hidden,
    lengths,
    key_cache,
    value_cache,
    gain_in,
    w_query,
    w_key,
    w_value,
    w_output,
    gain_post,
    w_gate,
    w_up,
    w_down,
):
    stream = hidden.astype(jnp.float32)
    squares = lax.psum(jnp.sum(stream * stream, axis=1), "kvseq")
    normed = (stream * lax.rsqrt(squares / D + epsilon)[:, None] * gain_in).astype(jnp.bfloat16)
    query_part = jnp.dot(normed, w_query, preferred_element_type=jnp.float32)
    key_part = jnp.dot(normed, w_key, preferred_element_type=jnp.float32)
    value_part = jnp.dot(normed, w_value, preferred_element_type=jnp.float32)
    query, key, value = lax.psum((query_part, key_part, value_part), "kvseq")
    seq_count = hidden.shape[0]
    query_heads = w_query.shape[1] // HD
    kv_heads = w_key.shape[1] // HD
    per_group = query_heads // kv_heads
    position = lengths.astype(jnp.float32)
    query = rotate(query.reshape(seq_count, query_heads, HD), position)
    new_keys = rotate(key.reshape(seq_count, kv_heads, HD), position).astype(jnp.bfloat16)
    new_values = value.reshape(seq_count, kv_heads, HD).astype(jnp.bfloat16)
    grouped = query.astype(jnp.bfloat16).reshape(seq_count, kv_heads, per_group, HD)
    local_len = key_cache.shape[1]
    cached_keys = key_cache.reshape(seq_count, local_len, kv_heads, HD)
    cached_values = value_cache.reshape(seq_count, local_len, kv_heads, HD)
    factor = float(HD) ** (-0.5)
    scores = (
        jnp.einsum("skgd,slkd->skgl", grouped, cached_keys, preferred_element_type=jnp.float32)
        * factor
    )
    offsets = lax.axis_index("kvseq") * local_len + jnp.arange(local_len, dtype=jnp.int32)
    valid = (offsets[None, :] < lengths[:, None])[:, None, None, :]
    masked = jnp.where(valid, scores, -1e30)
    local_top = jnp.max(masked, axis=-1)
    weights = jnp.where(valid, jnp.exp(masked - local_top[..., None]), 0.0)
    local_total = jnp.sum(weights, axis=-1)
    local_mixed = jnp.einsum(
        "skgl,slkd->skgd",
        weights.astype(jnp.bfloat16),
        cached_values,
        preferred_element_type=jnp.float32,
    )
    top, total, mixed = combined_all((local_top, local_total, local_mixed), "kvseq", combine_parts)
    own = (
        jnp.einsum("skgd,skd->skg", grouped, new_keys, preferred_element_type=jnp.float32) * factor
    )
    final_top = jnp.maximum(top, own)
    old_scale = jnp.exp(top - final_top)
    own_weight = jnp.exp(own - final_top)
    total = total * old_scale + own_weight
    mixed = (
        mixed * old_scale[..., None]
        + own_weight[..., None] * new_values.astype(jnp.float32)[:, :, None, :]
    )
    attended = (mixed / total[..., None]).astype(jnp.bfloat16).reshape(seq_count, query_heads * HD)
    projected = jnp.dot(attended, w_output, preferred_element_type=jnp.float32)
    residual = stream + lax.psum(projected, "tensor")
    squares_post = lax.psum(jnp.sum(residual * residual, axis=1), "kvseq")
    normed_post = (residual * lax.rsqrt(squares_post / D + epsilon)[:, None] * gain_post).astype(
        jnp.bfloat16
    )
    gate_part = jnp.dot(normed_post, w_gate, preferred_element_type=jnp.float32)
    upward_part = jnp.dot(normed_post, w_up, preferred_element_type=jnp.float32)
    gate, upward = lax.psum((gate_part, upward_part), "kvseq")
    inner = (jax.nn.silu(gate) * upward).astype(jnp.bfloat16)
    down_part = jnp.dot(inner, w_down, preferred_element_type=jnp.float32)
    output = (residual + lax.psum(down_part, "tensor")).astype(jnp.bfloat16)
    return (
        output,
        new_keys.reshape(seq_count, kv_heads * HD),
        new_values.reshape(seq_count, kv_heads * HD),
    )


def solution(mesh):
    placed = (
        P("groups", "kvseq"),
        P("groups"),
        P("groups", "kvseq", "tensor"),
        P("groups", "kvseq", "tensor"),
        P("kvseq"),
        P("kvseq", "tensor"),
        P("kvseq", "tensor"),
        P("kvseq", "tensor"),
        P("tensor", "kvseq"),
        P("kvseq"),
        P("kvseq", "tensor"),
        P("kvseq", "tensor"),
        P("tensor", "kvseq"),
    )
    return jax.shard_map(
        per_device,
        mesh=mesh,
        in_specs=placed,
        out_specs=(P("groups", "kvseq"), P("groups", "tensor"), P("groups", "tensor")),
        check_vma=False,
    )
```

profile of v0, /device:TPU:1, one launch (start us, length us, event | category | flops | bytes accessed | tf_op | source)
XLA Modules:
  0.0 336.3 jit_solution(1588148959176730858)
XLA Ops:
  7.2 0.0 copy-start
  7.2 0.0 copy-start.3
  7.2 0.0 copy-start.4
  7.2 0.0 all-reduce.5.cloned.1.call-start
  7.3 1.0 fusion.30
  8.3 18.7 %psum.63 = f32[8]{0:T(128)S(1)} all-reduce(f32[8]{0:T(128)S(1)} %fusion.30), channel_id=1, replica_groups=mesh['groups'=2,'kvseq'=8,'tensor'=2] {'kvseq'}, use_global_device_ids=true, to_apply=%region_1.0 | all-reduce | flops 8 | bytes 64 | tf_op jit(solution)/shard_map/psum | solution.py:69
  27.0 5.3 %convolution_bitcast_fusion = f32[8,32,128]{2,0,1:T(8,128)} fusion(bf16[1024,4096]{1,0:T(8,128)(2,1)} %param.20, bf16[8,1024]{1,0:T(8,128)(2,1)} %param.15, f32[1024]{0:T(1024)} %param.19, f32[8]{0:T(128)S(1)} %add_rsqrt_fusion.1), kind=kOutput, calls=%fused_computation.16 | convolution fusion | flops 67141632 | bytes 8540192 | tf_op jit(solution)/shard_map/dot_general | solution.py:71
  32.3 0.0 all-reduce.5.cloned.1.call-update
  32.3 0.0 all-reduce.7.cloned.1.call-start
  32.5 0.3 convolution_bitcast_fusion.1
  32.8 1.5 fusion.41
  34.3 26.2 %all-reduce = (f32[8,4,128]{2,0,1:T(8,128)S(1)}, bf16[8,512]{1,0:T(8,128)(2,1)S(1)}) all-reduce(f32[8,4,128]{2,0,1:T(8,128)S(1)} %convolution_bitcast_fusion.1, f32[8,512]{1,0:T(8,128)S(1)} %fusion.41), channel_id=1, replica_groups=mesh['groups'=2,'kvseq'=8,'tensor'=2] {'kvseq'}, use_global_device_ids=true, to_apply=%region_7.8 | all-reduce | flops 8192 | bytes 57344 | tf_op jit(solution)/shard_map/psum | solution.py:74
  60.4 0.1 multiply_cosine_fusion
  60.6 0.1 multiply_subtract_fusion
  60.6 0.1 broadcast_compare_fusion
  60.7 0.1 fusion.50
  60.8 41.2 %all-reduce.5.cloned.1.call-done = f32[8,32,128]{2,0,1:T(8,128)} async-done(((f32[8,32,128]{2,0,1:T(8,128)}), f32[8,32,128]{2,0,1:T(8,128)}) %all-reduce.5.cloned.1.call-update) | async-done | bytes 131088 | tf_op jit(solution)/shard_map/psum | solution.py:74
  102.0 1.1 subtract_convert_fusion
  103.2 0.2 fusion.35
  103.4 0.0 copy-done
  103.4 0.8 fusion.48
  104.2 0.2 fusion.19
  104.4 2.0 fusion.15
  106.4 24.8 %all-gather = bf16[64,4,8]{2,1,0:T(4,128)(2,1)S(1)} all-gather(bf16[8,4,8]{2,1,0:T(4,128)(2,1)S(1)} %convert_element_type.141), channel_id=2, replica_groups=mesh['groups'=2,'kvseq'=8,'tensor'=2] {'kvseq'}, dimensions={0}, use_global_device_ids=true | all-gather | bytes 4608 | tf_op jit(solution)/shard_map/all_gather | solution.py:16
  131.2 24.2 %all-gather.1 = bf16[64,4,8]{2,1,0:T(4,128)(2,1)S(1)} all-gather(bf16[8,4,8]{2,1,0:T(4,128)(2,1)S(1)} %fusion.19), channel_id=3, replica_groups=mesh['groups'=2,'kvseq'=8,'tensor'=2] {'kvseq'}, dimensions={0}, use_global_device_ids=true | all-gather | bytes 4608 | tf_op jit(solution)/shard_map/all_gather | solution.py:16
  155.4 25.7 %all-gather.2 = bf16[64,4,8,128]{3,2,1,0:T(8,128)(2,1)S(1)} all-gather(bf16[8,4,8,128]{3,2,1,0:T(8,128)(2,1)S(1)} %fusion.15), channel_id=4, replica_groups=mesh['groups'=2,'kvseq'=8,'tensor'=2] {'kvseq'}, dimensions={0}, use_global_device_ids=true | all-gather | bytes 589824 | tf_op jit(solution)/shard_map/all_gather | solution.py:16
  181.1 1.6 while.19
  181.2 0.2 fusion.67
  181.4 0.2 fusion.67
  181.6 0.2 fusion.67
  181.9 0.2 fusion.67
  182.1 0.2 fusion.67
  182.3 0.2 fusion.67
  182.5 0.2 fusion.67
  182.8 0.2 fusion.29
  182.9 4.6 %fusion.26 = f32[8,1024]{1,0:T(8,128)S(1)} fusion(bf16[4096,1024]{1,0:T(8,128)(2,1)} %param.23, bf16[1,8,32,128]{3,2,1,0:T(8,128)(2,1)S(1)} %fusion.29), kind=kOutput, calls=%fused_computation.31 | convolution fusion | flops 67108864 | bytes 8486912 | tf_op jit(solution)/shard_map/dot_general | solution.py:117
  187.5 23.4 %psum.67 = f32[8,1024]{1,0:T(8,128)S(1)} all-reduce(f32[8,1024]{1,0:T(8,128)S(1)} %fusion.26), channel_id=1, replica_groups=mesh['groups'=2,'kvseq'=8,'tensor'=2] {'tensor'}, use_global_device_ids=true, to_apply=%region_9.10 | all-reduce | flops 8192 | bytes 65536 | tf_op jit(solution)/shard_map/psum | solution.py:118
  211.0 0.1 multiply_reduce_fusion
  211.1 15.8 %psum.68 = f32[8]{0:T(128)S(1)} all-reduce(f32[8]{0:T(128)S(1)} %multiply_reduce_fusion), channel_id=1, replica_groups=mesh['groups'=2,'kvseq'=8,'tensor'=2] {'kvseq'}, use_global_device_ids=true, to_apply=%region_11.12 | all-reduce | flops 8 | bytes 64 | tf_op jit(solution)/shard_map/psum | solution.py:119
  226.9 0.1 multiply_convert_fusion.2
  227.0 8.3 %fusion.52 = f32[8,7680]{1,0:T(8,128)} fusion(bf16[8,1024]{1,0:T(8,128)(2,1)S(1)} %multiply_convert_fusion.2, bf16[1024,7680]{1,0:T(8,128)(2,1)} %param.26), kind=kOutput, calls=%fused_computation.77 | convolution fusion | flops 125829120 | bytes 15990784 | tf_op jit(solution)/shard_map/dot_general | solution.py:124
  235.3 8.3 %fusion.51 = f32[8,7680]{1,0:T(8,128)} fusion(bf16[8,1024]{1,0:T(8,128)(2,1)S(1)} %multiply_convert_fusion.2, bf16[1024,7680]{1,0:T(8,128)(2,1)} %param.25), kind=kOutput, calls=%fused_computation.76 | convolution fusion | flops 125829120 | bytes 15990784 | tf_op jit(solution)/shard_map/dot_general | solution.py:123
  243.6 0.0 all-reduce.7.cloned.1.call-update
  243.6 0.7 fusion.49
  244.3 70.4 %all-reduce.7.cloned.1.call-done = (f32[8,7680]{1,0:T(8,128)}, f32[8,7680]{1,0:T(8,128)}) async-done(((f32[8,7680]{1,0:T(8,128)}, f32[8,7680]{1,0:T(8,128)}), (f32[8,7680]{1,0:T(8,128)}, f32[8,7680]{1,0:T(8,128)})) %all-reduce.7.cloned.1.call-update) | async-done | bytes 491536 | tf_op jit(solution)/shard_map/psum | solution.py:125
  314.8 8.0 %fusion.24 = f32[8,1024]{1,0:T(8,128)S(1)} fusion(bf16[7680,1024]{1,0:T(8,128)(2,1)} %param.27, f32[8,7680]{1,0:T(8,128)} %get-tuple-element.200, f32[8,7680]{1,0:T(8,128)} %get-tuple-element.201), kind=kOutput, calls=%fused_computation.29 | convolution fusion | flops 126197760 | bytes 16252928 | tf_op jit(solution)/shard_map/dot_general | solution.py:127
  322.7 6.1 %psum.71 = f32[8,1024]{1,0:T(8,128)S(1)} all-reduce(f32[8,1024]{1,0:T(8,128)S(1)} %fusion.24), channel_id=1, replica_groups=mesh['groups'=2,'kvseq'=8,'tensor'=2] {'tensor'}, use_global_device_ids=true, to_apply=%region_14.15 | all-reduce | flops 8192 | bytes 65536 | tf_op jit(solution)/shard_map/psum | solution.py:128
  328.9 0.6 add_convert_fusion.1
  (32 shorter events, 0.4 us)
Async XLA Ops:
  7.2 96.2 %copy-start = (bf16[8,256,512]{2,1,0:T(8,128)(2,1)S(1)}, bf16[8,256,512]{2,1,0:T(8,128)(2,1)}, u32[]{:S(2)}) copy-start(bf16[8,256,512]{2,1,0:T(8,128)(2,1)} %param.17) | copy-start | bytes 6291460
  7.2 25.3 %copy-start.3 = (bf16[8,1024]{1,0:T(8,128)(2,1)S(1)}, bf16[8,1024]{1,0:T(8,128)(2,1)}, u32[]{:S(2)}) copy-start(bf16[8,1024]{1,0:T(8,128)(2,1)} %param.15) | copy-start | bytes 49156
  7.2 25.3 %copy-start.4 = (f32[1024]{0:T(1024)S(1)}, f32[1024]{0:T(1024)}, u32[]{:S(2)}) copy-start(f32[1024]{0:T(1024)} %param.19) | copy-start | bytes 12292
  7.2 25.2 %copy-start.7 = (s32[8]{0:T(128)S(1)}, s32[8]{0:T(128)}, u32[]{:S(2)}) copy-start(s32[8]{0:T(128)} %param.16) | copy-start | bytes 100
  7.2 25.2 %copy-start.2 = (bf16[1024,512]{1,0:T(8,128)(2,1)S(1)}, bf16[1024,512]{1,0:T(8,128)(2,1)}, u32[]{:S(2)}) copy-start(bf16[1024,512]{1,0:T(8,128)(2,1)} %param.21) | copy-start | bytes 3145732
  7.2 94.8 %all-reduce.5.cloned.1.call-start = ((), (), s32[]{:S(2)}) async-start(), calls=%async_computation | async-start | bytes 262144 | tf_op jit(solution)/shard_map/psum | solution.py:74
  32.3 282.4 %all-reduce.7.cloned.1.call-start = ((), (), s32[]{:S(2)}) async-start(), calls=%async_computation.1 | async-start | bytes 983040 | tf_op jit(solution)/shard_map/psum | solution.py:125
  60.4 127.1 %copy-start.5 = (bf16[8,512]{1,0:T(8,128)(2,1)}, bf16[8,512]{1,0:T(8,128)(2,1)S(1)}, u32[]{:S(2)}) copy-start(bf16[8,512]{1,0:T(8,128)(2,1)S(1)} %get-tuple-element.199) | copy-start | bytes 24580
  182.7 44.2 %copy-start.6 = (f32[1024]{0:T(1024)S(1)}, f32[1024]{0:T(1024)}, u32[]{:S(2)}) copy-start(f32[1024]{0:T(1024)} %param.24) | copy-start | bytes 12292
  314.8 14.7 %copy-start.1 = (bf16[8,256,512]{2,1,0:T(8,128)(2,1)S(1)}, bf16[8,256,512]{2,1,0:T(8,128)(2,1)}, u32[]{:S(2)}) copy-start(bf16[8,256,512]{2,1,0:T(8,128)(2,1)} %param.17) | copy-start | bytes 6291460
Sparse Core Ops, SparseCore 0:
  32.5 69.5 all-reduce.4
  243.8 70.9 all-reduce.6
where the time goes:
time: 337 us; the launch traced here: 336 us
  blocking collectives  165 us (49%)
  waiting for transfers between devices  112 us (33%)
  matrix products  39.3 us (12%)
  between operations  14.2 us (4%)
  other arithmetic  5.8 us (2%)
    all_gather x3, blocking collectives, combined_all(): lax.all_gather(a.astype(kind), axis)  74.6 us
    psum x1, waiting for transfers between devices, per_device(): gate, upward = lax.psum((gate_part, upward_part), 'kvseq')  70.4 us
    psum x1, waiting for transfers between devices, per_device(): query, key, value = lax.psum((query_part, key_part, value_part), 'kvseq')  41.2 us
    psum x1, blocking collectives, per_device(): query, key, value = lax.psum((query_part, key_part, value_part), 'kvseq')  26.2 us
    psum x1, blocking collectives, per_device(): residual = stream + lax.psum(projected, 'tensor')  23.4 us
    psum x1, blocking collectives, per_device(): squares = lax.psum(jnp.sum(stream * stream, axis=1), 'kvseq')  18.7 us
    psum x1, blocking collectives, per_device(): squares_post = lax.psum(jnp.sum(residual * residual, axis=1), 'kvseq')  15.8 us
    dot_general x1, matrix products, per_device(): upward_part = jnp.dot(normed_post, w_up, preferred_element_type=jnp.float32)  8.31 us
  transfers between devices with their start and end apart: 2, of which 2 were waited for; matrix products, arithmetic and copies ran while one was open for 1% of the time, Pallas kernels for 0%

commit v1 on v0

v1 whole, which is shorter than its diff:
```python
import functools

import jax
import jax.numpy as jnp
import numpy as np
from jax import lax
from jax.experimental import pallas as pl
from jax.experimental.pallas import tpu as pltpu
from jax.sharding import PartitionSpec as P

HD = 128
epsilon = 1e-06
rope_base = 1000000.0
BF = jnp.bfloat16
F32 = jnp.float32
MESH = pl.DeviceIdType.MESH


def mult(x, m):
    return pl.multiple_of(x, m)


def when(cond, f):
    if cond is True:
        f()
    else:
        pl.when(cond)(f)


def layer_kernel(
    c,
    lengths,
    hidden,
    gain_in,
    gain_post,
    freq,
    kc_hbm,
    vc_hbm,
    wq_hbm,
    wk_hbm,
    wv_hbm,
    wo_hbm,
    wg_hbm,
    wu_hbm,
    wd_hbm,
    out,
    new_keys,
    new_values,
    wqkv,
    tail,
    wo,
    wg,
    wu,
    kc,
    vc,
    send_a,
    recv_a,
    all_a,
    send_b,
    recv_b,
    send_m,
    recv_m,
    all_b,
    part_1,
    send_c,
    recv_c,
    all_c,
    part_2,
    wsem,
    dsem,
    sa_s,
    sa_r,
    ga_s,
    ga_r,
    sb_s,
    sb_r,
    sm_s,
    sm_r,
    gb_s,
    gb_r,
    t1_s,
    t1_r,
    sc_s,
    sc_r,
    gc_s,
    gc_r,
    t2_s,
    t2_r,
):
    n, T, A = c["n"], c["T"], c["A"]
    S, Dl, L = c["S"], c["Dl"], c["L"]
    QH, KH, W = c["QH"], c["KH"], c["W"]
    QC, KC = QH * HD, KH * HD
    TOT = QC + 2 * KC
    CA = TOT // A
    HA = CA // HD
    HB = QH // A
    CB = HB * HD
    FT = c["FT"]
    reuse = c["reuse"]
    per_group = QH // KH
    D = float(Dl * n)
    me = lax.axis_index("kvseq")
    t = lax.axis_index("tensor")
    owner = True if n == A else me < A

    def local(src, dst, sem):
        return pltpu.make_async_copy(src, dst, sem)

    first = [
        local(wq_hbm, wqkv.at[:, pl.ds(0, QC)], wsem.at[0]),
        local(wk_hbm, wqkv.at[:, pl.ds(QC, KC)], wsem.at[1]),
        local(wv_hbm, wqkv.at[:, pl.ds(QC + KC, KC)], wsem.at[2]),
    ]
    later = [
        local(kc_hbm, kc, wsem.at[3]),
        local(vc_hbm, vc, wsem.at[4]),
        local(wo_hbm, wo, wsem.at[5]),
        local(wg_hbm, wg, wsem.at[6]),
        local(wu_hbm, wu, wsem.at[7]),
    ]

    def down_slot(d):
        return wqkv.at[:, pl.ds(d * Dl, Dl)] if d < reuse else tail.at[d - reuse]

    down = [
        local(wd_hbm.at[pl.ds((d * FT // A) * HD, W), :], down_slot(d), dsem.at[d])
        for d in range(A)
    ]
    for x in first:
        x.start()

    barrier = pltpu.get_barrier_semaphore()

    def greet(k, _):
        pl.semaphore_signal(
            barrier, inc=1, device_id={"kvseq": lax.rem(me + k, n)}, device_id_type=MESH
        )
        return 0

    lax.fori_loop(1, n, greet, 0)
    for k in range(1, T):
        pl.semaphore_signal(
            barrier, inc=1, device_id={"tensor": lax.rem(t + k, T)}, device_id_type=MESH
        )

    def remote(src, dst, s_sem, r_sem, to):
        return pltpu.make_async_remote_copy(
            src_ref=src, dst_ref=dst, send_sem=s_sem, recv_sem=r_sem, device_id=to,
            device_id_type=MESH,
        )

    def scatter(send, recv, s_sem, r_sem, d):
        return remote(send.at[d], recv.at[me], s_sem.at[d], r_sem.at[me], {"kvseq": d})

    def scatter_wait_recv(send, recv, s_sem, r_sem):
        def one(k, _):
            src = lax.rem(me + k, n)
            remote(
                send.at[0], recv.at[src], s_sem.at[0], r_sem.at[src], {"kvseq": src}
            ).wait_recv()
            return 0

        lax.fori_loop(1, n, one, 0)

    def scatter_wait_send(send, recv, s_sem, r_sem):
        for d in range(A):
            pl.when(d != me)(lambda d=d: scatter(send, recv, s_sem, r_sem, d).wait_send())

    def gather_start(view, s_sem, r_sem):
        def one(k, _):
            to = lax.rem(me + k, n)
            remote(view(me), view(me), s_sem.at[k], r_sem.at[me], {"kvseq": to}).start()
            return 0

        lax.fori_loop(1, n, one, 0)

    def gather_wait_recv(view, s_sem, r_sem):
        def one(s, _):
            @pl.when(s != me)
            def _():
                remote(view(s), view(s), s_sem.at[0], r_sem.at[s], {"kvseq": s}).wait_recv()

            return 0

        lax.fori_loop(0, A, one, 0)

    def gather_wait_send(view, s_sem, r_sem):
        def one(k, _):
            to = lax.rem(me + k, n)
            remote(view(me), view(me), s_sem.at[k], r_sem.at[me], {"kvseq": to}).wait_send()
            return 0

        def run():
            lax.fori_loop(1, n, one, 0)

        when(owner, run)

    def pair_copies(part, s_sem, r_sem):
        return [
            remote(
                part.at[t], part.at[t], s_sem.at[k], r_sem.at[t], {"tensor": lax.rem(t + k, T)}
            )
            for k in range(1, T)
        ]

    def pair_sum(part, s_sem, r_sem):
        for x in pair_copies(part, s_sem, r_sem):
            x.start()
        for k in range(1, T):
            src = lax.rem(t + k, T)
            remote(
                part.at[src], part.at[src], s_sem.at[k], r_sem.at[src], {"tensor": src}
            ).wait_recv()
        total = part[0]
        for i in range(1, T):
            total = total + part[i]
        return total

    lane = lax.broadcasted_iota(jnp.int32, (S, HD), 1)
    row = lax.broadcasted_iota(jnp.int32, (S, HD), 0)

    def squares_block(x):
        s = jnp.broadcast_to(jnp.sum(x * x, axis=1, keepdims=True), (S, HD))
        high = s.astype(BF).astype(F32)
        return jnp.where(lane < HD // 2, high, s - high).astype(BF)

    def row_scale(block):
        total = jnp.sum(block, axis=1, keepdims=True) * (2.0 / HD)
        return lax.rsqrt(total / D + epsilon)

    stream = hidden[...].astype(F32)
    xg = (stream * gain_in[...]).astype(BF)
    sq = squares_block(stream)

    position = jnp.zeros((S, HD), F32)
    for s in range(S):
        position = jnp.where(row == s, lengths[s].astype(F32), position)
    angle = position * freq[...]
    cosine = jnp.cos(angle)
    sine = jnp.sin(angle)
    sine = jnp.where(lane < HD // 2, -sine, sine)

    for x in first:
        x.wait()
    for x in later + down[reuse:]:
        x.start()
    pl.semaphore_wait(barrier, (n - 1) + (T - 1))

    def project(k, _):
        d = lax.rem(me + 1 + k, A)
        part = jnp.dot(xg, wqkv[:, pl.ds(mult(d * CA, HD), CA)], preferred_element_type=F32)
        send_a[d, :, :CA] = part.astype(BF)
        send_a[d, :, CA:] = sq

        @pl.when(d != me)
        def _():
            scatter(send_a, recv_a, sa_s, sa_r, d).start()

        return 0

    lax.fori_loop(0, A, project, 0)
    for x in down[:reuse]:
        x.start()

    def view_a(s):
        return all_a.at[:, pl.ds(mult(s * CA, HD), CA)]

    def reduce_a():
        recv_a[me] = send_a[me]
        scatter_wait_recv(send_a, recv_a, sa_s, sa_r)
        total = lax.fori_loop(
            1, n, lambda s, acc: acc + recv_a[s].astype(F32), recv_a[0].astype(F32)
        )
        scale = row_scale(total[:, CA:])
        for j in range(HA):
            v = total[:, j * HD : (j + 1) * HD] * scale
            turned = v * cosine + pltpu.roll(v, HD // 2, 1) * sine
            rot = jnp.broadcast_to(me * HA + j, (S, HD)) < QH + KH
            res = jnp.where(rot, turned, v).astype(BF)
            all_a[:, pl.ds(mult((me * HA + j) * HD, HD), HD)] = res
        gather_start(view_a, ga_s, ga_r)

    when(owner, reduce_a)
    gather_wait_recv(view_a, ga_s, ga_r)
    new_keys[...] = all_a[:, QC : QC + KC]
    new_values[...] = all_a[:, QC + KC :]

    R = per_group * S
    brow = lax.broadcasted_iota(jnp.int32, (R, L), 0) % S
    orow = lax.broadcasted_iota(jnp.int32, (R, HD), 0) % S
    limit = jnp.zeros((R, L), jnp.int32)
    for s in range(S):
        limit = jnp.where(brow == s, lengths[s], limit)
    place = lax.broadcasted_iota(jnp.int32, (R, L), 1) + me * L
    valid = place < limit
    factor = float(HD) ** (-0.5)
    later[0].wait()
    later[1].wait()

    def attend(g, _):
        q = jnp.concatenate(
            [
                all_a[:, pl.ds(mult((g * per_group + j) * HD, HD), HD)].astype(F32)
                for j in range(per_group)
            ],
            axis=0,
        ).astype(BF)
        scores = jnp.zeros((R, L), F32)
        for s in range(S):
            keys = kc[s, :, pl.ds(mult(g * HD, HD), HD)]
            x = lax.dot_general(
                q, keys, (((1,), (1,)), ((), ())), preferred_element_type=F32
            )
            scores = jnp.where(brow == s, x, scores)
        scores = jnp.where(valid, scores * factor, -1e30)
        top = jnp.max(scores, axis=1, keepdims=True)
        w = jnp.where(valid, jnp.exp(scores - top), 0.0)
        total = jnp.sum(w, axis=1, keepdims=True)
        w = w.astype(BF)
        mixed = jnp.zeros((R, HD), F32)
        for s in range(S):
            vals = vc[s, :, pl.ds(mult(g * HD, HD), HD)]
            x = jnp.dot(w, vals, preferred_element_type=F32)
            mixed = jnp.where(orow == s, x, mixed)
        for i in range(per_group // HB):
            d = g * (per_group // HB) + i
            ml = jnp.zeros((S, HD), F32)
            for j in range(HB):
                r = (i * HB + j) * S
                send_b[d, :, j * HD : (j + 1) * HD] = mixed[r : r + S].astype(BF)
                ml = jnp.where(lane == j, top[r : r + S], ml)
                ml = jnp.where(lane == HD // 2 + j, total[r : r + S], ml)
            send_m[d] = ml

            @pl.when(d != me)
            def _():
                scatter(send_b, recv_b, sb_s, sb_r, d).start()
                scatter(send_m, recv_m, sm_s, sm_r, d).start()

        return 0

    lax.fori_loop(0, KH, attend, 0)

    def view_b(s):
        return all_b.at[:, pl.ds(mult(s * CB, HD), CB)]

    def reduce_b():
        recv_b[me] = send_b[me]
        recv_m[me] = send_m[me]
        scatter_wait_recv(send_m, recv_m, sm_s, sm_r)
        top = lax.fori_loop(1, n, lambda s, acc: jnp.maximum(acc, recv_m[s]), recv_m[0])
        scatter_wait_recv(send_b, recv_b, sb_s, sb_r)

        def join(s, state):
            total, mixed = state
            m = recv_m[s]
            scale = jnp.exp(m - top)
            total = total + pltpu.roll(m, HD // 2, 1) * scale
            x = recv_b[s].astype(F32)
            mixed = tuple(
                mixed[j] + x[:, j * HD : (j + 1) * HD] * scale[:, j : j + 1] for j in range(HB)
            )
            return total, mixed

        zero = jnp.zeros((S, HD), F32)
        total, mixed = lax.fori_loop(0, n, join, (zero, (zero,) * HB))
        for j in range(HB):
            h = me * HB + j
            g = h // per_group
            q = all_a[:, pl.ds(mult(h * HD, HD), HD)].astype(F32)
            key = all_a[:, pl.ds(mult(QC + g * HD, HD), HD)].astype(F32)
            val = all_a[:, pl.ds(mult(QC + KC + g * HD, HD), HD)].astype(F32)
            own = jnp.sum(q * key, axis=1, keepdims=True) * factor
            old = top[:, j : j + 1]
            best = jnp.maximum(old, own)
            old_scale = jnp.exp(old - best)
            own_weight = jnp.exp(own - best)
            bottom = total[:, j : j + 1] * old_scale + own_weight
            res = (mixed[j] * old_scale + own_weight * val) / bottom
            all_b[:, pl.ds(mult(h * HD, HD), HD)] = res.astype(BF)
        gather_start(view_b, gb_s, gb_r)

    when(owner, reduce_b)
    gather_wait_recv(view_b, gb_s, gb_r)

    NB = min(256, Dl)
    later[2].wait()

    def output_tile(j, _):
        cols = pl.ds(mult(j * NB, NB), NB)
        part_1[t, :, cols] = jnp.dot(all_b[...], wo[:, cols], preferred_element_type=F32)
        return 0

    lax.fori_loop(0, Dl // NB, output_tile, 0)
    residual = hidden[...].astype(F32) + pair_sum(part_1, t1_s, t1_r)
    sq_post = squares_block(residual)
    rg = (residual * gain_post[...]).astype(BF)
    later[3].wait()
    later[4].wait()

    def widen(k, _):
        d = lax.rem(me + 1 + k, A)
        begin = (d * FT // A) * HD
        for i, w in enumerate((wg, wu)):
            for j in range(0, W, 256):
                step = min(256, W - j)
                x = jnp.dot(
                    rg, w[:, pl.ds(mult(begin + j, HD), step)], preferred_element_type=F32
                )
                send_c[d, :, i * W + j : i * W + j + step] = x.astype(BF)
        send_c[d, :, 2 * W :] = sq_post

        @pl.when(d != me)
        def _():
            scatter(send_c, recv_c, sc_s, sc_r, d).start()

        return 0

    lax.fori_loop(0, A, widen, 0)

    def view_c(s):
        return all_c.at[s]

    def reduce_c():
        recv_c[me] = send_c[me]
        scatter_wait_recv(send_c, recv_c, sc_s, sc_r)
        total = lax.fori_loop(
            1, n, lambda s, acc: acc + recv_c[s].astype(F32), recv_c[0].astype(F32)
        )
        scale = row_scale(total[:, 2 * W :])
        gate = total[:, :W] * scale
        up = total[:, W : 2 * W] * scale
        inner = gate * jax.nn.sigmoid(gate) * up
        owned = ((me + 1) * FT // A - me * FT // A) * HD
        col = lax.broadcasted_iota(jnp.int32, (S, W), 1)
        all_c[me] = jnp.where(col < owned, inner, 0.0).astype(BF)
        gather_start(view_c, gc_s, gc_r)

    when(owner, reduce_c)
    for x in down:
        x.wait()
    gather_wait_recv(view_c, gc_s, gc_r)

    def down_tile(j, _):
        acc = jnp.zeros((S, NB), F32)
        for d in range(A):
            if d < reuse:
                w = wqkv[:, pl.ds(mult(d * Dl + j * NB, HD), NB)]
            else:
                w = tail[d - reuse, :, pl.ds(mult(j * NB, NB), NB)]
            acc = acc + jnp.dot(all_c[d], w, preferred_element_type=F32)
        part_2[t, :, pl.ds(mult(j * NB, NB), NB)] = acc
        return 0

    lax.fori_loop(0, Dl // NB, down_tile, 0)
    out[...] = (residual + pair_sum(part_2, t2_s, t2_r)).astype(BF)

    scatter_wait_send(send_a, recv_a, sa_s, sa_r)
    gather_wait_send(view_a, ga_s, ga_r)
    scatter_wait_send(send_b, recv_b, sb_s, sb_r)
    scatter_wait_send(send_m, recv_m, sm_s, sm_r)
    gather_wait_send(view_b, gb_s, gb_r)
    scatter_wait_send(send_c, recv_c, sc_s, sc_r)
    gather_wait_send(view_c, gc_s, gc_r)
    for part, s_sem, r_sem in ((part_1, t1_s, t1_r), (part_2, t2_s, t2_r)):
        for x in pair_copies(part, s_sem, r_sem):
            x.wait_send()


def per_device(
    n,
    T,
    hidden,
    lengths,
    key_cache,
    value_cache,
    gain_in,
    w_query,
    w_key,
    w_value,
    w_output,
    gain_post,
    w_gate,
    w_up,
    w_down,
):
    S, Dl = hidden.shape
    L = key_cache.shape[1]
    QC, KC = w_query.shape[1], w_key.shape[1]
    QH, KH = QC // HD, KC // HD
    FT = w_gate.shape[1] // HD
    A = max(
        a
        for a in range(1, n + 1)
        if n % a == 0
        and (QH + 2 * KH) % a == 0
        and QH % a == 0
        and (QH // KH) % (QH // a) == 0
        and a <= FT
    )
    W = -(-FT // A) * HD
    TOT = QC + 2 * KC
    reuse = min(A, TOT // Dl) if Dl == W else 0
    c = dict(n=n, T=T, A=A, S=S, Dl=Dl, L=L, QH=QH, KH=KH, W=W, FT=FT, reuse=reuse)
    CA, CB = TOT // A, QC // A
    CC = 2 * W + HD
    half = np.arange(HD) % (HD // 2)
    freq = jnp.asarray((rope_base ** (-half * 2.0 / HD)).astype(np.float32)[None, :])
    dma = pltpu.SemaphoreType.DMA
    V = pltpu.VMEM
    anywhere = pl.BlockSpec(memory_space=pl.ANY)
    vmem = pl.BlockSpec(memory_space=pltpu.VMEM)
    smem = pl.BlockSpec(memory_space=pltpu.SMEM)
    return pl.pallas_call(
        functools.partial(layer_kernel, c),
        out_shape=(
            jax.ShapeDtypeStruct((S, Dl), BF),
            jax.ShapeDtypeStruct((S, KC), BF),
            jax.ShapeDtypeStruct((S, KC), BF),
        ),
        in_specs=[smem] + [vmem] * 4 + [anywhere] * 9,
        out_specs=(vmem,) * 3,
        scratch_shapes=[
            V((Dl, TOT), BF),
            V((max(A - reuse, 1), W, Dl), BF),
            V((QC, Dl), BF),
            V((Dl, FT * HD), BF),
            V((Dl, FT * HD), BF),
            V(key_cache.shape, BF),
            V(value_cache.shape, BF),
            V((A, S, CA + HD), BF),
            V((n, S, CA + HD), BF),
            V((S, TOT), BF),
            V((A, S, CB), BF),
            V((n, S, CB), BF),
            V((A, S, HD), F32),
            V((n, S, HD), F32),
            V((S, QC), BF),
            V((T, S, Dl), F32),
            V((A, S, CC), BF),
            V((n, S, CC), BF),
            V((A, S, W), BF),
            V((T, S, Dl), F32),
            dma((8,)),
            dma((A,)),
            dma((A,)),
            dma((n,)),
            dma((n,)),
            dma((A,)),
            dma((A,)),
            dma((n,)),
            dma((A,)),
            dma((n,)),
            dma((n,)),
            dma((A,)),
            dma((T,)),
            dma((T,)),
            dma((A,)),
            dma((n,)),
            dma((n,)),
            dma((A,)),
            dma((T,)),
            dma((T,)),
        ],
        compiler_params=pltpu.CompilerParams(
            collective_id=0, has_side_effects=True, vmem_limit_bytes=67000000
        ),
    )(
        lengths,
        hidden,
        gain_in[None, :],
        gain_post[None, :],
        freq,
        key_cache,
        value_cache,
        w_query,
        w_key,
        w_value,
        w_output,
        w_gate,
        w_up,
        w_down,
    )


def solution(mesh):
    placed = (
        P("groups", "kvseq"),
        P("groups"),
        P("groups", "kvseq", "tensor"),
        P("groups", "kvseq", "tensor"),
        P("kvseq"),
        P("kvseq", "tensor"),
        P("kvseq", "tensor"),
        P("kvseq", "tensor"),
        P("tensor", "kvseq"),
        P("kvseq"),
        P("kvseq", "tensor"),
        P("kvseq", "tensor"),
        P("tensor", "kvseq"),
    )
    return jax.shard_map(
        functools.partial(per_device, mesh.shape["kvseq"], mesh.shape["tensor"]),
        mesh=mesh,
        in_specs=placed,
        out_specs=(P("groups", "kvseq"), P("groups", "tensor"), P("groups", "tensor")),
        check_vma=False,
    )
```

time: 337 us -> 55.8 us (0.17)
  blocking collectives: 165 us -> 0 us
  waiting for transfers between devices: 112 us -> 0 us
  Pallas kernels: 0 us -> 50.9 us
  matrix products: 39.3 us -> 0 us
  between operations: 14.2 us -> 0.65 us
  other arithmetic: 5.8 us -> 0 us
  local copies, waits for them, and re-layouts: 0.07 us -> 3.91 us
    psum x2 -> x0, waiting for transfers between devices: 112 us -> none  [the longest x1 70.4 us: per_device(): gate, upward = lax.psum((gate_part, upward_part), 'kvseq')]
    psum x5 -> x0, blocking collectives: 90.3 us -> none  [the longest x1 26.2 us: per_device(): query, key, value = lax.psum((query_part, key_part, value_part), 'kvseq')]
    all_gather x3 -> x0, blocking collectives: 74.6 us -> none  [combined_all(): lax.all_gather(a.astype(kind), axis)]
    pallas_call x0 -> x1, Pallas kernels: none -> 50.9 us  [per_device(): pl.pallas_call(functools.partial(layer_kernel, c), out_shape=(jax.ShapeDt...]
    dot_general x10 -> x0, matrix products: 39.3 us -> none  [the longest x1 8.31 us: per_device(): upward_part = jnp.dot(normed_post, w_up, preferred_element_type=jnp.float32)]
    unnamed x16 -> x3, local copies, waits for them, and re-layouts: 0.05 us -> 3.91 us
  transfers between devices with their start and end apart: 2 -> 0, of which waited for: 2 -> 0; matrix products, arithmetic and copies ran while one was open for 1% -> 0% of each run, Pallas kernels for 0% -> 0%
where the time goes in v1:
time: 55.8 us; the launch traced here: 55.4 us
  Pallas kernels  50.9 us (91%)
  local copies, waits for them, and re-layouts  3.91 us (7%)
  between operations  0.65 us (1%)
    pallas_call x1, Pallas kernels, per_device(): pl.pallas_call(functools.partial(layer_kernel, c), out_shape=(jax.ShapeDt...  50.9 us
    unnamed x3, local copies, waits for them, and re-layouts  3.91 us

profile of v1, /device:TPU:1, one launch (start us, length us, event | category | flops | bytes accessed | tf_op | source)
XLA Modules:
  0.0 55.4 jit_solution(15988980837496045816)
XLA Ops:
  0.6 50.9 %shard_map.157 = (bf16[8,1024]{1,0:T(8,128)(2,1)}, bf16[8,512]{1,0:T(8,128)(2,1)}, bf16[8,512]{1,0:T(8,128)(2,1)}) custom-call(s32[8]{0:T(128)} %lengths.1, bf16[8,1024]{1,0:T(8,128)(2,1)} %hidden.1, f32[1,1024]{1,0:T(1,128)} %bitcast.2, f32[1,1024]{1,0:T(1,128)} %bitcast.3, f32[1,128]{1,0:T(1,128)} %constant.2.clone.freq, bf16[8,256,512]{2,1,0:T(8,128)(2,1)} %kc_hbm.1, ...), custom_call_target="tpu_custom_call" | custom-call | tf_op jit(solution)/shard_map/pallas_call | solution.py:515
  51.5 1.3 %copy.20 = bf16[8,1024]{1,0:T(8,128)(2,1)} copy(bf16[8,1024]{1,0:T(8,128)(2,1)} %get-tuple-element.6) | data formatting | bytes 32768
  52.8 1.3 %copy.21 = bf16[8,512]{1,0:T(8,128)(2,1)} copy(bf16[8,512]{1,0:T(8,128)(2,1)} %get-tuple-element.7) | data formatting | bytes 16384
  54.1 1.3 %copy.22 = bf16[8,512]{1,0:T(8,128)(2,1)} copy(bf16[8,512]{1,0:T(8,128)(2,1)} %get-tuple-element.8) | data formatting | bytes 16384

commit v2 on v1

--- a/solution.py
+++ b/solution.py
@@ -27,13 +27,20 @@
         pl.when(cond)(f)
 
 
+def split_kernel(packed, out, new_keys, new_values):
+    Dl, KC = out.shape[1], new_keys.shape[1]
+    out[...] = packed[:, :Dl]
+    new_keys[...] = packed[:, Dl : Dl + KC]
+    new_values[...] = packed[:, Dl + KC :]
+
+
 def layer_kernel(
     c,
-    lengths,
-    hidden,
-    gain_in,
-    gain_post,
-    freq,
+    lengths_hbm,
+    hidden_hbm,
+    gain_in_hbm,
+    gain_post_hbm,
+    freq_hbm,
     kc_hbm,
     vc_hbm,
     wq_hbm,
@@ -44,8 +51,11 @@
     wu_hbm,
     wd_hbm,
     out,
-    new_keys,
-    new_values,
+    lengths,
+    hidden,
+    gain_in,
+    gain_post,
+    freq,
     wqkv,
     tail,
     wo,
@@ -53,6 +63,7 @@
     wu,
     kc,
     vc,
+    early_a,
     send_a,
     recv_a,
     all_a,
@@ -67,6 +78,7 @@
     all_c,
     part_2,
     wsem,
+    fsem,
     dsem,
     sa_s,
     sa_r,
@@ -107,10 +119,17 @@
     def local(src, dst, sem):
         return pltpu.make_async_copy(src, dst, sem)
 
+    half = Dl // 2
     first = [
-        local(wq_hbm, wqkv.at[:, pl.ds(0, QC)], wsem.at[0]),
-        local(wk_hbm, wqkv.at[:, pl.ds(QC, KC)], wsem.at[1]),
-        local(wv_hbm, wqkv.at[:, pl.ds(QC + KC, KC)], wsem.at[2]),
+        local(
+            src.at[pl.ds(b * half, half), :],
+            wqkv.at[pl.ds(b * half, half), pl.ds(at, width)],
+            fsem.at[b * 3 + i],
+        )
+        for b in range(2)
+        for i, (src, at, width) in enumerate(
+            ((wq_hbm, 0, QC), (wk_hbm, QC, KC), (wv_hbm, QC + KC, KC))
+        )
     ]
     later = [
         local(kc_hbm, kc, wsem.at[3]),
@@ -127,7 +146,14 @@
         local(wd_hbm.at[pl.ds((d * FT // A) * HD, W), :], down_slot(d), dsem.at[d])
         for d in range(A)
     ]
-    for x in first:
+    small = [
+        local(lengths_hbm, lengths, wsem.at[8]),
+        local(hidden_hbm, hidden, wsem.at[9]),
+        local(gain_in_hbm, gain_in, wsem.at[10]),
+        local(gain_post_hbm, gain_post, wsem.at[11]),
+        local(freq_hbm, freq, wsem.at[12]),
+    ]
+    for x in small + first:
         x.start()
 
     barrier = pltpu.get_barrier_semaphore()
@@ -174,6 +200,9 @@
             return 0
 
         lax.fori_loop(1, n, one, 0)
+
+    def gather_one(view, s_sem, r_sem, s):
+        remote(view(s), view(s), s_sem.at[0], r_sem.at[s], {"kvseq": s}).wait_recv()
 
     def gather_wait_recv(view, s_sem, r_sem):
         def one(s, _):
@@ -229,6 +258,14 @@
         total = jnp.sum(block, axis=1, keepdims=True) * (2.0 / HD)
         return lax.rsqrt(total / D + epsilon)
 
+    def far_first(k):
+        return lax.rem(me + A // 2 + ((k + 1) // 2) * (1 - 2 * (k % 2)) + A, A)
+
+    def near_first(k):
+        return far_first(A - 1 - k)
+
+    for x in small:
+        x.wait()
     stream = hidden[...].astype(F32)
     xg = (stream * gain_in[...]).astype(BF)
     sq = squares_block(stream)
@@ -241,15 +278,26 @@
     sine = jnp.sin(angle)
     sine = jnp.where(lane < HD // 2, -sine, sine)
 
-    for x in first:
+    for x in first[:3]:
+        x.wait()
+    def project_early(d, _):
+        cols = pl.ds(mult(d * CA, HD), CA)
+        early_a[d] = jnp.dot(xg[:, :half], wqkv[:half, cols], preferred_element_type=F32)
+        return 0
+
+    lax.fori_loop(0, A, project_early, 0)
+    for x in first[3:]:
         x.wait()
     for x in later + down[reuse:]:
         x.start()
     pl.semaphore_wait(barrier, (n - 1) + (T - 1))
 
     def project(k, _):
-        d = lax.rem(me + 1 + k, A)
-        part = jnp.dot(xg, wqkv[:, pl.ds(mult(d * CA, HD), CA)], preferred_element_type=F32)
+        d = far_first(k)
+        cols = pl.ds(mult(d * CA, HD), CA)
+        part = early_a[d] + jnp.dot(
+            xg[:, half:], wqkv[half:, cols], preferred_element_type=F32
+        )
         send_a[d, :, :CA] = part.astype(BF)
         send_a[d, :, CA:] = sq
 
@@ -283,8 +331,7 @@
 
     when(owner, reduce_a)
     gather_wait_recv(view_a, ga_s, ga_r)
-    new_keys[...] = all_a[:, QC : QC + KC]
-    new_values[...] = all_a[:, QC + KC :]
+    out[:, Dl:] = all_a[:, QC:]
 
     R = per_group * S
     brow = lax.broadcasted_iota(jnp.int32, (R, L), 0) % S
@@ -382,17 +429,21 @@
         gather_start(view_b, gb_s, gb_r)
 
     when(owner, reduce_b)
-    gather_wait_recv(view_b, gb_s, gb_r)
-
-    NB = min(256, Dl)
     later[2].wait()
-
-    def output_tile(j, _):
-        cols = pl.ds(mult(j * NB, NB), NB)
-        part_1[t, :, cols] = jnp.dot(all_b[...], wo[:, cols], preferred_element_type=F32)
+    part_1[t] = jnp.zeros((S, Dl), F32)
+
+    def output_block(k, _):
+        d = near_first(k)
+
+        @pl.when(d != me)
+        def _():
+            gather_one(view_b, gb_s, gb_r, d)
+
+        x = all_b[:, pl.ds(mult(d * CB, HD), CB)]
+        part_1[t] += jnp.dot(x, wo[pl.ds(mult(d * CB, HD), CB), :], preferred_element_type=F32)
         return 0
 
-    lax.fori_loop(0, Dl // NB, output_tile, 0)
+    lax.fori_loop(0, A, output_block, 0)
     residual = hidden[...].astype(F32) + pair_sum(part_1, t1_s, t1_r)
     sq_post = squares_block(residual)
     rg = (residual * gain_post[...]).astype(BF)
@@ -400,7 +451,7 @@
     later[4].wait()
 
     def widen(k, _):
-        d = lax.rem(me + 1 + k, A)
+        d = far_first(k)
         begin = (d * FT // A) * HD
         for i, w in enumerate((wg, wu)):
             for j in range(0, W, 256):
@@ -440,21 +491,34 @@
     when(owner, reduce_c)
     for x in down:
         x.wait()
-    gather_wait_recv(view_c, gc_s, gc_r)
-
-    def down_tile(j, _):
-        acc = jnp.zeros((S, NB), F32)
-        for d in range(A):
-            if d < reuse:
-                w = wqkv[:, pl.ds(mult(d * Dl + j * NB, HD), NB)]
-            else:
-                w = tail[d - reuse, :, pl.ds(mult(j * NB, NB), NB)]
-            acc = acc + jnp.dot(all_c[d], w, preferred_element_type=F32)
-        part_2[t, :, pl.ds(mult(j * NB, NB), NB)] = acc
+    part_2[t] = jnp.zeros((S, Dl), F32)
+
+    def down_block(k, _):
+        d = near_first(k)
+
+        @pl.when(d != me)
+        def _():
+            gather_one(view_c, gc_s, gc_r, d)
+
+        x = all_c[d]
+        if reuse:
+
+            @pl.when(d < reuse)
+            def _():
+                w = wqkv[:, pl.ds(mult(d * Dl, HD), Dl)]
+                part_2[t] += jnp.dot(x, w, preferred_element_type=F32)
+
+        if reuse < A:
+
+            @pl.when(d >= reuse)
+            def _():
+                w = tail[jnp.maximum(d - reuse, 0)]
+                part_2[t] += jnp.dot(x, w, preferred_element_type=F32)
+
         return 0
 
-    lax.fori_loop(0, Dl // NB, down_tile, 0)
-    out[...] = (residual + pair_sum(part_2, t2_s, t2_r)).astype(BF)
+    lax.fori_loop(0, A, down_block, 0)
+    out[:, :Dl] = (residual + pair_sum(part_2, t2_s, t2_r)).astype(BF)
 
     scatter_wait_send(send_a, recv_a, sa_s, sa_r)
     gather_wait_send(view_a, ga_s, ga_r)
@@ -511,17 +575,17 @@
     V = pltpu.VMEM
     anywhere = pl.BlockSpec(memory_space=pl.ANY)
     vmem = pl.BlockSpec(memory_space=pltpu.VMEM)
-    smem = pl.BlockSpec(memory_space=pltpu.SMEM)
-    return pl.pallas_call(
+    packed = pl.pallas_call(
         functools.partial(layer_kernel, c),
-        out_shape=(
-            jax.ShapeDtypeStruct((S, Dl), BF),
-            jax.ShapeDtypeStruct((S, KC), BF),
-            jax.ShapeDtypeStruct((S, KC), BF),
-        ),
-        in_specs=[smem] + [vmem] * 4 + [anywhere] * 9,
-        out_specs=(vmem,) * 3,
+        out_shape=jax.ShapeDtypeStruct((S, Dl + 2 * KC), BF),
+        in_specs=[anywhere] * 14,
+        out_specs=vmem,
         scratch_shapes=[
+            pltpu.SMEM(lengths.shape, jnp.int32),
+            V((S, Dl), BF),
+            V((1, Dl), F32),
+            V((1, Dl), F32),
+            V((1, HD), F32),
             V((Dl, TOT), BF),
             V((max(A - reuse, 1), W, Dl), BF),
             V((QC, Dl), BF),
@@ -529,6 +593,7 @@
             V((Dl, FT * HD), BF),
             V(key_cache.shape, BF),
             V(value_cache.shape, BF),
+            V((A, S, CA), F32),
             V((A, S, CA + HD), BF),
             V((n, S, CA + HD), BF),
             V((S, TOT), BF),
@@ -542,7 +607,8 @@
             V((n, S, CC), BF),
             V((A, S, W), BF),
             V((T, S, Dl), F32),
-            dma((8,)),
+            dma((13,)),
+            dma((6,)),
             dma((A,)),
             dma((A,)),
             dma((n,)),
@@ -582,6 +648,16 @@
         w_up,
         w_down,
     )
+    return pl.pallas_call(
+        split_kernel,
+        out_shape=(
+            jax.ShapeDtypeStruct((S, Dl), BF),
+            jax.ShapeDtypeStruct((S, KC), BF),
+            jax.ShapeDtypeStruct((S, KC), BF),
+        ),
+        in_specs=[vmem],
+        out_specs=(vmem,) * 3,
+    )(packed)
 
 
 def solution(mesh):

time: 55.8 us -> 51.9 us (0.930)
  local copies, waits for them, and re-layouts: 3.91 us -> 0 us
    unnamed x3 -> x0, local copies, waits for them, and re-layouts: 3.91 us -> none
    pallas_call x1 -> x2, Pallas kernels: 50.9 us -> 51 us  [the longest x1 49.7 us: per_device(): pl.pallas_call(functools.partial(layer_kernel, c), out_shape=jax.ShapeDty...]
where the time goes in v2:
time: 51.9 us; the launch traced here: 51.7 us
  Pallas kernels  51 us (98%)
  between operations  0.64 us (1%)
    pallas_call x1, Pallas kernels, per_device(): pl.pallas_call(functools.partial(layer_kernel, c), out_shape=jax.ShapeDty...  49.7 us
    pallas_call x1, Pallas kernels, per_device(): pl.pallas_call(split_kernel, out_shape=(jax.ShapeDtypeStruct((S, Dl), BF)...  1.37 us

profile of v2, /device:TPU:1, one launch (start us, length us, event | category | flops | bytes accessed | tf_op | source)
XLA Modules:
  0.0 51.7 jit_solution(7633281373908146659)
XLA Ops:
  0.6 49.7 %shard_map.157.packed = bf16[8,2048]{1,0:T(8,128)(2,1)} custom-call(s32[8]{0:T(128)} %lengths_hbm.1, bf16[8,1024]{1,0:T(8,128)(2,1)} %hidden_hbm.1, f32[1,1024]{1,0:T(1,128)} %bitcast.2, f32[1,1024]{1,0:T(1,128)} %bitcast.3, f32[1,128]{1,0:T(1,128)} %constant.2.clone.freq_hbm, bf16[8,256,512]{2,1,0:T(8,128)(2,1)} %kc_hbm.1, bf16[8,256,512]{2,1,0:T(8,128)(2,1)} %vc_hbm.1, ...), custom_call_target="tpu_custom_call" | custom-call | tf_op jit(solution)/shard_map/pallas_call | solution.py:578
  50.3 1.4 %shard_map.158 = (bf16[8,1024]{1,0:T(8,128)(2,1)}, bf16[8,512]{1,0:T(8,128)(2,1)}, bf16[8,512]{1,0:T(8,128)(2,1)}) custom-call(bf16[8,2048]{1,0:T(8,128)(2,1)} %shard_map.157.packed), custom_call_target="tpu_custom_call" | custom-call | tf_op jit(solution)/shard_map/pallas_call | solution.py:651

commit v3 on v2

--- a/solution.py
+++ b/solution.py
@@ -72,10 +72,12 @@
     send_m,
     recv_m,
     all_b,
+    acc_1,
     part_1,
     send_c,
     recv_c,
     all_c,
+    acc_2,
     part_2,
     wsem,
     fsem,
@@ -193,9 +195,14 @@
         for d in range(A):
             pl.when(d != me)(lambda d=d: scatter(send, recv, s_sem, r_sem, d).wait_send())
 
+    def gather_to(k):
+        if n % 2:
+            return lax.rem(me + k, n)
+        return lax.rem(me + n // 2 + (k // 2) * (1 - 2 * ((k + 1) % 2)) + n, n)
+
     def gather_start(view, s_sem, r_sem):
         def one(k, _):
-            to = lax.rem(me + k, n)
+            to = gather_to(k)
             remote(view(me), view(me), s_sem.at[k], r_sem.at[me], {"kvseq": to}).start()
             return 0
 
@@ -216,7 +223,7 @@
 
     def gather_wait_send(view, s_sem, r_sem):
         def one(k, _):
-            to = lax.rem(me + k, n)
+            to = gather_to(k)
             remote(view(me), view(me), s_sem.at[k], r_sem.at[me], {"kvseq": to}).wait_send()
             return 0
 
@@ -233,7 +240,8 @@
             for k in range(1, T)
         ]
 
-    def pair_sum(part, s_sem, r_sem):
+    def pair_sum(acc, part, s_sem, r_sem):
+        part[t] = acc[...].astype(BF)
         for x in pair_copies(part, s_sem, r_sem):
             x.start()
         for k in range(1, T):
@@ -241,9 +249,9 @@
             remote(
                 part.at[src], part.at[src], s_sem.at[k], r_sem.at[src], {"tensor": src}
             ).wait_recv()
-        total = part[0]
+        total = part[0].astype(F32)
         for i in range(1, T):
-            total = total + part[i]
+            total = total + part[i].astype(F32)
         return total
 
     lane = lax.broadcasted_iota(jnp.int32, (S, HD), 1)
@@ -430,7 +438,7 @@
 
     when(owner, reduce_b)
     later[2].wait()
-    part_1[t] = jnp.zeros((S, Dl), F32)
+    acc_1[...] = jnp.zeros((S, Dl), F32)
 
     def output_block(k, _):
         d = near_first(k)
@@ -440,11 +448,11 @@
             gather_one(view_b, gb_s, gb_r, d)
 
         x = all_b[:, pl.ds(mult(d * CB, HD), CB)]
-        part_1[t] += jnp.dot(x, wo[pl.ds(mult(d * CB, HD), CB), :], preferred_element_type=F32)
+        acc_1[...] += jnp.dot(x, wo[pl.ds(mult(d * CB, HD), CB), :], preferred_element_type=F32)
         return 0
 
     lax.fori_loop(0, A, output_block, 0)
-    residual = hidden[...].astype(F32) + pair_sum(part_1, t1_s, t1_r)
+    residual = hidden[...].astype(F32) + pair_sum(acc_1, part_1, t1_s, t1_r)
     sq_post = squares_block(residual)
     rg = (residual * gain_post[...]).astype(BF)
     later[3].wait()
@@ -491,7 +499,7 @@
     when(owner, reduce_c)
     for x in down:
         x.wait()
-    part_2[t] = jnp.zeros((S, Dl), F32)
+    acc_2[...] = jnp.zeros((S, Dl), F32)
 
     def down_block(k, _):
         d = near_first(k)
@@ -506,19 +514,19 @@
             @pl.when(d < reuse)
             def _():
                 w = wqkv[:, pl.ds(mult(d * Dl, HD), Dl)]
-                part_2[t] += jnp.dot(x, w, preferred_element_type=F32)
+                acc_2[...] += jnp.dot(x, w, preferred_element_type=F32)
 
         if reuse < A:
 
             @pl.when(d >= reuse)
             def _():
                 w = tail[jnp.maximum(d - reuse, 0)]
-                part_2[t] += jnp.dot(x, w, preferred_element_type=F32)
+                acc_2[...] += jnp.dot(x, w, preferred_element_type=F32)
 
         return 0
 
     lax.fori_loop(0, A, down_block, 0)
-    out[:, :Dl] = (residual + pair_sum(part_2, t2_s, t2_r)).astype(BF)
+    out[:, :Dl] = (residual + pair_sum(acc_2, part_2, t2_s, t2_r)).astype(BF)
 
     scatter_wait_send(send_a, recv_a, sa_s, sa_r)
     gather_wait_send(view_a, ga_s, ga_r)
@@ -602,11 +610,13 @@
             V((A, S, HD), F32),
             V((n, S, HD), F32),
             V((S, QC), BF),
-            V((T, S, Dl), F32),
+            V((S, Dl), F32),
+            V((T, S, Dl), BF),
             V((A, S, CC), BF),
             V((n, S, CC), BF),
             V((A, S, W), BF),
-            V((T, S, Dl), F32),
+            V((S, Dl), F32),
+            V((T, S, Dl), BF),
             dma((13,)),
             dma((6,)),
             dma((A,)),

time: 51.9 us -> 53.7 us (1.035)
  Pallas kernels: 51 us -> 52.9 us
    pallas_call x1, Pallas kernels: 49.7 us -> 51.5 us  [per_device(): pl.pallas_call(functools.partial(layer_kernel, c), out_shape=jax.ShapeDty...]
where the time goes in v3:
time: 53.7 us; the launch traced here: 53.5 us
  Pallas kernels  52.9 us (99%)
  between operations  0.64 us (1%)
    pallas_call x1, Pallas kernels, per_device(): pl.pallas_call(functools.partial(layer_kernel, c), out_shape=jax.ShapeDty...  51.5 us
    pallas_call x1, Pallas kernels, per_device(): pl.pallas_call(split_kernel, out_shape=(jax.ShapeDtypeStruct((S, Dl), BF)...  1.37 us

profile of v3, /device:TPU:1, one launch (start us, length us, event | category | flops | bytes accessed | tf_op | source)
XLA Modules:
  0.0 53.5 jit_solution(10916773894917005118)
XLA Ops:
  0.6 51.5 %shard_map.157.packed = bf16[8,2048]{1,0:T(8,128)(2,1)} custom-call(s32[8]{0:T(128)} %lengths_hbm.1, bf16[8,1024]{1,0:T(8,128)(2,1)} %hidden_hbm.1, f32[1,1024]{1,0:T(1,128)} %bitcast.2, f32[1,1024]{1,0:T(1,128)} %bitcast.3, f32[1,128]{1,0:T(1,128)} %constant.2.clone.freq_hbm, bf16[8,256,512]{2,1,0:T(8,128)(2,1)} %kc_hbm.1, bf16[8,256,512]{2,1,0:T(8,128)(2,1)} %vc_hbm.1, ...), custom_call_target="tpu_custom_call" | custom-call | tf_op jit(solution)/shard_map/pallas_call | solution.py:586
  52.1 1.4 %shard_map.158 = (bf16[8,1024]{1,0:T(8,128)(2,1)}, bf16[8,512]{1,0:T(8,128)(2,1)}, bf16[8,512]{1,0:T(8,128)(2,1)}) custom-call(bf16[8,2048]{1,0:T(8,128)(2,1)} %shard_map.157.packed), custom_call_target="tpu_custom_call" | custom-call | tf_op jit(solution)/shard_map/pallas_call | solution.py:661
